TPU v7x, 32 devices: a whole 2x2x4 slice. The times are simulated.
32 devices in a mesh: row: 4 (over z), col: 8 (over y, x, core).
Axes of the slice: x: 2, y: 2, z: 4, core: 2. Of those that a mesh axis runs over, the one named last changes fastest.
Arguments:
- rhs: float32 [64, 131072], P(None, ('row', 'col')), may hold values from -6 to 6
- pivots: int32 [4096], replicated, may hold values from 0 to 131071, as said below
- factor: float32 [4096, 4, 8, 128], P('row', None, 'col'), as said below
- diag_inv: float32 [8, 512, 512], P('row'), as said below
Outputs:
- solution: float32 [64, 4, 8, 128], P(None, None, 'col')
Inputs may be any that keep to these rules, and one draw needn't show every extreme that they name: `pivots`: distinct column numbers, the first 4096 entries of a permutation of 0 .. 131071. `factor`: entry (row i, column q) is zero where q >= 512 * (i // 512). `diag_inv`: each block is unit lower triangular.
All inputs are finite; a program needn't handle non-finite values.
Results may differ from a plain program's by a relative error of at most 0.0001.
Values sent between devices are 32-bit elements; how exact they have to be, the bound alone decides.
A program may use at most 64 MiB of HBM per device.

v0:
```python
import jax
import jax.numpy as jnp
from jax import lax
from jax.sharding import PartitionSpec as P


def broadcast(shard, axis, root):
    mine = lax.axis_index(axis) == root
    return lax.psum(jnp.where(mine, shard, jnp.zeros_like(shard)), axis)


def apply_inverse(values, block_inv):
    return lax.dot_general(
        values,
        block_inv,
        (((1,), (1,)), ((), ())),
        precision=lax.Precision.HIGHEST,
        preferred_element_type=jnp.float32,
    )


def per_device(rhs, pivots, factor, diag_inv):
    my_row = lax.axis_index("row")
    my_col = lax.axis_index("col")
    col_count = lax.axis_size("col")
    rhs_count = rhs.shape[0]
    slab_rows = factor.shape[0]
    rounds = factor.shape[1]
    piece_len = factor.shape[3]
    block_len = diag_inv.shape[1]
    pieces = block_len // piece_len
    blocks_here = slab_rows // block_len
    total_blocks = blocks_here * lax.axis_size("row")
    first_column = (my_row * col_count + my_col) * rhs.shape[1]
    source_len = rhs.shape[1]
    located = pivots - first_column
    inside = (located >= 0) & (located < source_len)
    taken = jnp.take(rhs, jnp.clip(located, 0, source_len - 1), axis=1)
    taken = jnp.where(inside[None, :], taken, 0.0)
    permuted = lax.psum_scatter(
        jnp.transpose(
            taken.reshape(rhs_count, blocks_here * lax.axis_size("row"), block_len), (1, 0, 2)
        ),
        "row",
        scatter_dimension=0,
        tiled=True,
    )
    permuted = lax.psum(permuted, "col")
    factor_rows = factor.reshape(slab_rows, rounds * piece_len)

    def advance(number, solved):
        owner_row = number // blocks_here
        local_block = number % blocks_here
        block_rows = lax.dynamic_slice_in_dim(factor_rows, local_block * block_len, block_len, 0)
        partial_value = lax.dot_general(
            solved.reshape(rhs_count, rounds * piece_len),
            block_rows,
            (((1,), (1,)), ((), ())),
            precision=lax.Precision.HIGHEST,
            preferred_element_type=jnp.float32,
        )
        own_rhs = lax.dynamic_index_in_dim(permuted, local_block, 0, keepdims=False)
        block_inv = lax.dynamic_index_in_dim(diag_inv, local_block, 0, keepdims=False)
        summed = lax.psum(partial_value, "col")
        fresh = apply_inverse(own_rhs - summed, block_inv)
        fresh = broadcast(fresh, "row", owner_row)
        first_piece = number * pieces
        offset_piece = (my_col - first_piece) % col_count
        owns = offset_piece < pieces
        which = jnp.clip(offset_piece, 0, pieces - 1)
        local_round = jnp.clip((first_piece + offset_piece) // col_count, 0, rounds - 1)
        piece = lax.dynamic_slice_in_dim(fresh, which * piece_len, piece_len, 1)
        updated = lax.dynamic_update_index_in_dim(solved, piece[:, None, :], local_round, 1)
        return jnp.where(owns, updated, solved)

    start_state = jnp.zeros((rhs_count, rounds, 1, piece_len), jnp.float32)
    return lax.fori_loop(0, total_blocks, advance, start_state)


def solution(mesh):
    return jax.shard_map(
        per_device,
        mesh=mesh,
        in_specs=(P(None, ("row", "col")), P(), P("row", None, "col", None), P("row", None, None)),
        out_specs=P(None, None, "col", None),
        check_vma=False,
    )
```

profile of v0, /device:TPU:0, one launch (start us, length us, event | category | flops | bytes accessed | tf_op | source)
XLA Modules:
  0.0 882.2 jit_solution(17491685887215917001)
XLA Ops:
  8.1 1.8 copy.8
  9.9 14.1 %gather_fusion = f32[4096,64]{1,0:T(8,128)} fusion(f32[64,4096]{0,1:T(8,128)S(1)} %copy.8, s32[4096]{0:T(1024)S(1)} %fusion.8), kind=kCustom, calls=%fused_computation | custom fusion | bytes 2113536 | tf_op jit(solution)/shard_map/jit(_take)/gather | solution.py:38
  24.0 2.2 copy.9
  27.4 30.1 %reduce-scatter.2.cloned.1.call-done = f32[2,64,512]{2,1,0:T(8,128)} async-done(((f32[8,64,512]{2,1,0:T(8,128)}), f32[2,64,512]{2,1,0:T(8,128)}) %reduce-scatter.2.cloned.1.call-update) | async-done | bytes 262160 | tf_op jit(solution)/shard_map/reduce_scatter | solution.py:40
  59.3 53.7 %all-reduce.4.cloned.1.call-done = f32[2,64,512]{2,1,0:T(8,128)} async-done(((f32[2,64,512]{2,1,0:T(8,128)}), f32[2,64,512]{2,1,0:T(8,128)}) %all-reduce.4.cloned.1.call-update) | async-done | bytes 262160 | tf_op jit(solution)/shard_map/psum | solution.py:48
  113.0 761.7 %while.16 = (s32[]{:T(128)}, f32[64,4,1,128]{3,1,0,2:T(4,128)S(1)}, s32[]{:T(128)}, f32[2,64,512]{2,1,0:T(8,128)}, f32[1024,512]{1,0:T(8,128)S(1)}, /*index=5*/f...) while((s32[]{:T(128)}, f32[64,4,1,128]{3,1,0,2:T(4,128)S(1)}, ...), condition=%wide.region_5.6_spmd, body=%wide.region_2.5_spmd.sunk | while | flops 402792448 | bytes 4557184 | solution.py:77
  115.0 54.8 %all-reduce.6.cloned.1.call-done = f32[64,512]{1,0:T(8,128)} async-done(((f32[64,512]{1,0:T(8,128)}), f32[64,512]{1,0:T(8,128)}) %all-reduce.6.cloned.1.call-update) | async-done | bytes 131088 | tf_op jit(solution)/shard_map/while/body/eval_jaxpr/psum | solution.py:64
  169.7 3.1 convolution_select_fusion.2
  172.9 34.1 %all-reduce.8.cloned.1.call-done = f32[64,512]{1,0:T(8,128)} async-done(((f32[64,512]{1,0:T(8,128)}), f32[64,512]{1,0:T(8,128)}) %all-reduce.8.cloned.1.call-update) | async-done | bytes 131088 | tf_op jit(solution)/shard_map/while/body/eval_jaxpr/psum | solution.py:9
  208.1 1.8 convolution_bitcast_fusion.2
  210.0 54.8 %all-reduce.6.cloned.1.call-done = f32[64,512]{1,0:T(8,128)} async-done(((f32[64,512]{1,0:T(8,128)}), f32[64,512]{1,0:T(8,128)}) %all-reduce.6.cloned.1.call-update) | async-done | bytes 131088 | tf_op jit(solution)/shard_map/while/body/eval_jaxpr/psum | solution.py:64
  264.8 3.1 convolution_select_fusion.2
  268.0 34.1 %all-reduce.8.cloned.1.call-done = f32[64,512]{1,0:T(8,128)} async-done(((f32[64,512]{1,0:T(8,128)}), f32[64,512]{1,0:T(8,128)}) %all-reduce.8.cloned.1.call-update) | async-done | bytes 131088 | tf_op jit(solution)/shard_map/while/body/eval_jaxpr/psum | solution.py:9
  305.1 55.1 %all-reduce.6.cloned.1.call-done = f32[64,512]{1,0:T(8,128)} async-done(((f32[64,512]{1,0:T(8,128)}), f32[64,512]{1,0:T(8,128)}) %all-reduce.6.cloned.1.call-update) | async-done | bytes 131088 | tf_op jit(solution)/shard_map/while/body/eval_jaxpr/psum | solution.py:64
  360.1 3.1 convolution_select_fusion.2
  363.3 34.1 %all-reduce.8.cloned.1.call-done = f32[64,512]{1,0:T(8,128)} async-done(((f32[64,512]{1,0:T(8,128)}), f32[64,512]{1,0:T(8,128)}) %all-reduce.8.cloned.1.call-update) | async-done | bytes 131088 | tf_op jit(solution)/shard_map/while/body/eval_jaxpr/psum | solution.py:9
  400.4 55.1 %all-reduce.6.cloned.1.call-done = f32[64,512]{1,0:T(8,128)} async-done(((f32[64,512]{1,0:T(8,128)}), f32[64,512]{1,0:T(8,128)}) %all-reduce.6.cloned.1.call-update) | async-done | bytes 131088 | tf_op jit(solution)/shard_map/while/body/eval_jaxpr/psum | solution.py:64
  455.5 3.1 convolution_select_fusion.2
  458.7 34.1 %all-reduce.8.cloned.1.call-done = f32[64,512]{1,0:T(8,128)} async-done(((f32[64,512]{1,0:T(8,128)}), f32[64,512]{1,0:T(8,128)}) %all-reduce.8.cloned.1.call-update) | async-done | bytes 131088 | tf_op jit(solution)/shard_map/while/body/eval_jaxpr/psum | solution.py:9
  495.8 55.1 %all-reduce.6.cloned.1.call-done = f32[64,512]{1,0:T(8,128)} async-done(((f32[64,512]{1,0:T(8,128)}), f32[64,512]{1,0:T(8,128)}) %all-reduce.6.cloned.1.call-update) | async-done | bytes 131088 | tf_op jit(solution)/shard_map/while/body/eval_jaxpr/psum | solution.py:64
  550.9 3.1 convolution_select_fusion.2
  554.1 34.1 %all-reduce.8.cloned.1.call-done = f32[64,512]{1,0:T(8,128)} async-done(((f32[64,512]{1,0:T(8,128)}), f32[64,512]{1,0:T(8,128)}) %all-reduce.8.cloned.1.call-update) | async-done | bytes 131088 | tf_op jit(solution)/shard_map/while/body/eval_jaxpr/psum | solution.py:9
  589.3 1.8 convolution_bitcast_fusion.2
  591.1 55.1 %all-reduce.6.cloned.1.call-done = f32[64,512]{1,0:T(8,128)} async-done(((f32[64,512]{1,0:T(8,128)}), f32[64,512]{1,0:T(8,128)}) %all-reduce.6.cloned.1.call-update) | async-done | bytes 131088 | tf_op jit(solution)/shard_map/while/body/eval_jaxpr/psum | solution.py:64
  646.2 3.1 convolution_select_fusion.2
  649.4 34.1 %all-reduce.8.cloned.1.call-done = f32[64,512]{1,0:T(8,128)} async-done(((f32[64,512]{1,0:T(8,128)}), f32[64,512]{1,0:T(8,128)}) %all-reduce.8.cloned.1.call-update) | async-done | bytes 131088 | tf_op jit(solution)/shard_map/while/body/eval_jaxpr/psum | solution.py:9
  686.5 54.8 %all-reduce.6.cloned.1.call-done = f32[64,512]{1,0:T(8,128)} async-done(((f32[64,512]{1,0:T(8,128)}), f32[64,512]{1,0:T(8,128)}) %all-reduce.6.cloned.1.call-update) | async-done | bytes 131088 | tf_op jit(solution)/shard_map/while/body/eval_jaxpr/psum | solution.py:64
  741.3 3.1 convolution_select_fusion.2
  744.5 34.1 %all-reduce.8.cloned.1.call-done = f32[64,512]{1,0:T(8,128)} async-done(((f32[64,512]{1,0:T(8,128)}), f32[64,512]{1,0:T(8,128)}) %all-reduce.8.cloned.1.call-update) | async-done | bytes 131088 | tf_op jit(solution)/shard_map/while/body/eval_jaxpr/psum | solution.py:9
  781.6 54.8 %all-reduce.6.cloned.1.call-done = f32[64,512]{1,0:T(8,128)} async-done(((f32[64,512]{1,0:T(8,128)}), f32[64,512]{1,0:T(8,128)}) %all-reduce.6.cloned.1.call-update) | async-done | bytes 131088 | tf_op jit(solution)/shard_map/while/body/eval_jaxpr/psum | solution.py:64
  836.3 3.1 convolution_select_fusion.2
  839.5 34.1 %all-reduce.8.cloned.1.call-done = f32[64,512]{1,0:T(8,128)} async-done(((f32[64,512]{1,0:T(8,128)}), f32[64,512]{1,0:T(8,128)}) %all-reduce.8.cloned.1.call-update) | async-done | bytes 131088 | tf_op jit(solution)/shard_map/while/body/eval_jaxpr/psum | solution.py:9
  (75 shorter events, 24.8 us)
Async XLA Ops:
  6.5 51.0 %reduce-scatter.2.cloned.1.call-start = ((), (), s32[]{:S(2)}) async-start(), calls=%async_computation.1 | async-start | bytes 1310720 | tf_op jit(solution)/shard_map/reduce_scatter | solution.py:40
  27.3 85.6 %all-reduce.4.cloned.1.call-start = ((), (), s32[]{:S(2)}) async-start(), calls=%async_computation.2 | async-start | bytes 524288 | tf_op jit(solution)/shard_map/psum | solution.py:48
  113.0 56.7 %all-reduce.6.cloned.1.call-start = ((), (), s32[]{:S(2)}) async-start(), calls=%async_computation.3 | async-start | bytes 262144 | tf_op jit(solution)/shard_map/while/body/eval_jaxpr/psum | solution.py:64
  114.9 92.2 %all-reduce.8.cloned.1.call-start = ((), (), s32[]{:S(2)}) async-start(), calls=%async_computation.4 | async-start | bytes 262144 | tf_op jit(solution)/shard_map/while/body/eval_jaxpr/psum | solution.py:9
  208.1 56.7 %all-reduce.6.cloned.1.call-start = ((), (), s32[]{:S(2)}) async-start(), calls=%async_computation.3 | async-start | bytes 262144 | tf_op jit(solution)/shard_map/while/body/eval_jaxpr/psum | solution.py:64
  209.9 92.2 %all-reduce.8.cloned.1.call-start = ((), (), s32[]{:S(2)}) async-start(), calls=%async_computation.4 | async-start | bytes 262144 | tf_op jit(solution)/shard_map/while/body/eval_jaxpr/psum | solution.py:9
  303.1 57.0 %all-reduce.6.cloned.1.call-start = ((), (), s32[]{:S(2)}) async-start(), calls=%async_computation.3 | async-start | bytes 262144 | tf_op jit(solution)/shard_map/while/body/eval_jaxpr/psum | solution.py:64
  305.0 92.5 %all-reduce.8.cloned.1.call-start = ((), (), s32[]{:S(2)}) async-start(), calls=%async_computation.4 | async-start | bytes 262144 | tf_op jit(solution)/shard_map/while/body/eval_jaxpr/psum | solution.py:9
  398.5 57.0 %all-reduce.6.cloned.1.call-start = ((), (), s32[]{:S(2)}) async-start(), calls=%async_computation.3 | async-start | bytes 262144 | tf_op jit(solution)/shard_map/while/body/eval_jaxpr/psum | solution.py:64
  400.4 92.5 %all-reduce.8.cloned.1.call-start = ((), (), s32[]{:S(2)}) async-start(), calls=%async_computation.4 | async-start | bytes 262144 | tf_op jit(solution)/shard_map/while/body/eval_jaxpr/psum | solution.py:9
  493.8 57.0 %all-reduce.6.cloned.1.call-start = ((), (), s32[]{:S(2)}) async-start(), calls=%async_computation.3 | async-start | bytes 262144 | tf_op jit(solution)/shard_map/while/body/eval_jaxpr/psum | solution.py:64
  495.7 92.5 %all-reduce.8.cloned.1.call-start = ((), (), s32[]{:S(2)}) async-start(), calls=%async_computation.4 | async-start | bytes 262144 | tf_op jit(solution)/shard_map/while/body/eval_jaxpr/psum | solution.py:9
  589.2 57.0 %all-reduce.6.cloned.1.call-start = ((), (), s32[]{:S(2)}) async-start(), calls=%async_computation.3 | async-start | bytes 262144 | tf_op jit(solution)/shard_map/while/body/eval_jaxpr/psum | solution.py:64
  591.1 92.5 %all-reduce.8.cloned.1.call-start = ((), (), s32[]{:S(2)}) async-start(), calls=%async_computation.4 | async-start | bytes 262144 | tf_op jit(solution)/shard_map/while/body/eval_jaxpr/psum | solution.py:9
  684.6 56.7 %all-reduce.6.cloned.1.call-start = ((), (), s32[]{:S(2)}) async-start(), calls=%async_computation.3 | async-start | bytes 262144 | tf_op jit(solution)/shard_map/while/body/eval_jaxpr/psum | solution.py:64
  686.4 92.2 %all-reduce.8.cloned.1.call-start = ((), (), s32[]{:S(2)}) async-start(), calls=%async_computation.4 | async-start | bytes 262144 | tf_op jit(solution)/shard_map/while/body/eval_jaxpr/psum | solution.py:9
  779.6 56.7 %all-reduce.6.cloned.1.call-start = ((), (), s32[]{:S(2)}) async-start(), calls=%async_computation.3 | async-start | bytes 262144 | tf_op jit(solution)/shard_map/while/body/eval_jaxpr/psum | solution.py:64
  781.5 92.2 %all-reduce.8.cloned.1.call-start = ((), (), s32[]{:S(2)}) async-start(), calls=%async_computation.4 | async-start | bytes 262144 | tf_op jit(solution)/shard_map/while/body/eval_jaxpr/psum | solution.py:9
  874.7 0.7 copy-start
Sparse Core Ops, SparseCore 0:
  27.5 29.9 reduce-scatter.1
  60.5 52.3 all-reduce.3
  116.8 52.8 all-reduce.5
  173.0 34.0 all-reduce.7
  211.6 53.1 all-reduce.5
  268.0 34.0 all-reduce.7
  307.0 53.1 all-reduce.5
  363.4 34.0 all-reduce.7
  402.3 53.1 all-reduce.5
  458.8 34.0 all-reduce.7
  497.7 53.1 all-reduce.5
  554.1 34.0 all-reduce.7
  593.0 53.1 all-reduce.5
  649.5 34.0 all-reduce.7
  688.1 53.1 all-reduce.5
  744.6 34.0 all-reduce.7
  783.2 53.1 all-reduce.5
  839.6 34.0 all-reduce.7
where the time goes:
time: 883 us; the launch traced here: 882 us
  waiting for transfers between devices  796 us (90%)
  matrix products  39.5 us (4%)
  local copies, waits for them, and re-layouts  28 us (3%)
  between operations  13.5 us (2%)
    psum x8, waiting for transfers between devices, advance(): summed = lax.psum(partial_value, 'col')  439 us
    psum x8, waiting for transfers between devices, broadcast(): return lax.psum(jnp.where(mine, shard, jnp.zeros_like(shard)), axis)  273 us
    psum x1, waiting for transfers between devices, per_device(): permuted = lax.psum(permuted, 'col')  53.7 us
    reduce_scatter x1, waiting for transfers between devices, per_device(): lax.psum_scatter(jnp.transpose(taken.reshape(rhs_count, blocks_here * lax...  30.1 us
    dot_general x8, matrix products, apply_inverse(): lax.dot_general(values, block_inv, (((1,), (1,)), ((), ())), precision=la...  25.1 us
  transfers between devices with their start and end apart: 18, of which 18 were waited for; matrix products, arithmetic and copies ran while one was open for 0% of the time, Pallas kernels for 0%

commit v1 on v0

--- a/solution.py
+++ b/solution.py
@@ -45,7 +45,9 @@
         scatter_dimension=0,
         tiled=True,
     )
-    permuted = lax.psum(permuted, "col")
+    permuted = permuted
+    for hop in (1, 2, 4):
+        permuted = permuted + lax.ppermute(permuted, "col", [(dev, dev ^ hop) for dev in range(8)])
     factor_rows = factor.reshape(slab_rows, rounds * piece_len)
 
     def advance(number, solved):

time: 883 us -> 844 us (0.956)
  waiting for transfers between devices: 796 us -> 754 us
    psum x1 -> x0, waiting for transfers between devices: 53.7 us -> none  [per_device(): permuted = lax.psum(permuted, 'col')]
    ppermute x0 -> x3, waiting for transfers between devices: none -> 12.8 us  [per_device(): lax.ppermute(permuted, 'col', [(dev, dev ^ hop) for dev in range(8)])]
  transfers between devices with their start and end apart: 18 -> 20, of which waited for: 18 -> 20; matrix products, arithmetic and copies ran while one was open for 0% -> 0% of each run, Pallas kernels for 0% -> 0%
where the time goes in v1:
time: 844 us; the launch traced here: 843 us
  waiting for transfers between devices  754 us (89%)
  matrix products  39 us (5%)
  local copies, waits for them, and re-layouts  28.1 us (3%)
  between operations  13.2 us (2%)
    psum x8, waiting for transfers between devices, advance(): summed = lax.psum(partial_value, 'col')  437 us
    psum x8, waiting for transfers between devices, broadcast(): return lax.psum(jnp.where(mine, shard, jnp.zeros_like(shard)), axis)  273 us
    reduce_scatter x1, waiting for transfers between devices, per_device(): lax.psum_scatter(jnp.transpose(taken.reshape(rhs_count, blocks_here * lax...  30.2 us
    dot_general x8, matrix products, apply_inverse(): lax.dot_general(values, block_inv, (((1,), (1,)), ((), ())), precision=la...  24.5 us
  transfers between devices with their start and end apart: 20, of which 20 were waited for; matrix products, arithmetic and copies ran while one was open for 0% of the time, Pallas kernels for 0%

profile of v1, /device:TPU:0, one launch (start us, length us, event | category | flops | bytes accessed | tf_op | source)
XLA Modules:
  0.0 842.9 jit_solution(13034769948467477972)
XLA Ops:
  8.1 1.8 copy.8
  9.9 14.2 %gather_fusion = f32[4096,64]{1,0:T(8,128)} fusion(f32[64,4096]{0,1:T(8,128)S(1)} %copy.8, s32[4096]{0:T(1024)S(1)} %fusion.8), kind=kCustom, calls=%fused_computation | custom fusion | bytes 2113536 | tf_op jit(solution)/shard_map/jit(_take)/gather | solution.py:38
  24.1 2.2 copy.9
  27.5 30.2 %reduce-scatter.2.cloned.1.call-done = f32[2,64,512]{2,1,0:T(8,128)} async-done(((f32[8,64,512]{2,1,0:T(8,128)}), f32[2,64,512]{2,1,0:T(8,128)}) %reduce-scatter.2.cloned.1.call-update) | async-done | bytes 262160 | tf_op jit(solution)/shard_map/reduce_scatter | solution.py:40
  61.9 6.9 collective-permute-done.1
  72.1 4.2 collective-permute-done.2
  76.4 759.3 %while.16 = (s32[]{:T(128)}, f32[64,4,1,128]{3,1,0,2:T(4,128)S(1)}, s32[]{:T(128)}, f32[2,64,512]{2,1,0:T(8,128)S(1)}, f32[1024,512]{1,0:T(8,128)S(1)}, /*index=...) while((s32[]{:T(128)}, f32[64,4,1,128]{3,1,0,2:T(4,128)S(1)}, ...), condition=%wide.region_4.5_spmd, body=%wide.region_1.4_spmd.sunk | while | flops 402792448 | bytes 4557184 | solution.py:79
  78.4 53.9 %all-reduce.3.cloned.1.call-done = f32[64,512]{1,0:T(8,128)} async-done(((f32[64,512]{1,0:T(8,128)}), f32[64,512]{1,0:T(8,128)}) %all-reduce.3.cloned.1.call-update) | async-done | bytes 131088 | tf_op jit(solution)/shard_map/while/body/eval_jaxpr/psum | solution.py:66
  132.3 3.1 convolution_select_fusion.2
  135.4 34.1 %all-reduce.5.cloned.1.call-done = f32[64,512]{1,0:T(8,128)} async-done(((f32[64,512]{1,0:T(8,128)}), f32[64,512]{1,0:T(8,128)}) %all-reduce.5.cloned.1.call-update) | async-done | bytes 131088 | tf_op jit(solution)/shard_map/while/body/eval_jaxpr/psum | solution.py:9
  172.5 54.8 %all-reduce.3.cloned.1.call-done = f32[64,512]{1,0:T(8,128)} async-done(((f32[64,512]{1,0:T(8,128)}), f32[64,512]{1,0:T(8,128)}) %all-reduce.3.cloned.1.call-update) | async-done | bytes 131088 | tf_op jit(solution)/shard_map/while/body/eval_jaxpr/psum | solution.py:66
  227.3 3.1 convolution_select_fusion.2
  230.4 34.1 %all-reduce.5.cloned.1.call-done = f32[64,512]{1,0:T(8,128)} async-done(((f32[64,512]{1,0:T(8,128)}), f32[64,512]{1,0:T(8,128)}) %all-reduce.5.cloned.1.call-update) | async-done | bytes 131088 | tf_op jit(solution)/shard_map/while/body/eval_jaxpr/psum | solution.py:9
  265.6 1.8 convolution_bitcast_fusion.2
  267.5 54.8 %all-reduce.3.cloned.1.call-done = f32[64,512]{1,0:T(8,128)} async-done(((f32[64,512]{1,0:T(8,128)}), f32[64,512]{1,0:T(8,128)}) %all-reduce.3.cloned.1.call-update) | async-done | bytes 131088 | tf_op jit(solution)/shard_map/while/body/eval_jaxpr/psum | solution.py:66
  322.3 3.1 convolution_select_fusion.2
  325.4 34.1 %all-reduce.5.cloned.1.call-done = f32[64,512]{1,0:T(8,128)} async-done(((f32[64,512]{1,0:T(8,128)}), f32[64,512]{1,0:T(8,128)}) %all-reduce.5.cloned.1.call-update) | async-done | bytes 131088 | tf_op jit(solution)/shard_map/while/body/eval_jaxpr/psum | solution.py:9
  362.5 55.1 %all-reduce.3.cloned.1.call-done = f32[64,512]{1,0:T(8,128)} async-done(((f32[64,512]{1,0:T(8,128)}), f32[64,512]{1,0:T(8,128)}) %all-reduce.3.cloned.1.call-update) | async-done | bytes 131088 | tf_op jit(solution)/shard_map/while/body/eval_jaxpr/psum | solution.py:66
  417.5 3.1 convolution_select_fusion.2
  420.7 34.1 %all-reduce.5.cloned.1.call-done = f32[64,512]{1,0:T(8,128)} async-done(((f32[64,512]{1,0:T(8,128)}), f32[64,512]{1,0:T(8,128)}) %all-reduce.5.cloned.1.call-update) | async-done | bytes 131088 | tf_op jit(solution)/shard_map/while/body/eval_jaxpr/psum | solution.py:9
  457.8 54.8 %all-reduce.3.cloned.1.call-done = f32[64,512]{1,0:T(8,128)} async-done(((f32[64,512]{1,0:T(8,128)}), f32[64,512]{1,0:T(8,128)}) %all-reduce.3.cloned.1.call-update) | async-done | bytes 131088 | tf_op jit(solution)/shard_map/while/body/eval_jaxpr/psum | solution.py:66
  512.5 3.1 convolution_select_fusion.2
  515.7 34.1 %all-reduce.5.cloned.1.call-done = f32[64,512]{1,0:T(8,128)} async-done(((f32[64,512]{1,0:T(8,128)}), f32[64,512]{1,0:T(8,128)}) %all-reduce.5.cloned.1.call-update) | async-done | bytes 131088 | tf_op jit(solution)/shard_map/while/body/eval_jaxpr/psum | solution.py:9
  552.8 54.8 %all-reduce.3.cloned.1.call-done = f32[64,512]{1,0:T(8,128)} async-done(((f32[64,512]{1,0:T(8,128)}), f32[64,512]{1,0:T(8,128)}) %all-reduce.3.cloned.1.call-update) | async-done | bytes 131088 | tf_op jit(solution)/shard_map/while/body/eval_jaxpr/psum | solution.py:66
  607.5 3.1 convolution_select_fusion.2
  610.7 34.1 %all-reduce.5.cloned.1.call-done = f32[64,512]{1,0:T(8,128)} async-done(((f32[64,512]{1,0:T(8,128)}), f32[64,512]{1,0:T(8,128)}) %all-reduce.5.cloned.1.call-update) | async-done | bytes 131088 | tf_op jit(solution)/shard_map/while/body/eval_jaxpr/psum | solution.py:9
  647.7 54.8 %all-reduce.3.cloned.1.call-done = f32[64,512]{1,0:T(8,128)} async-done(((f32[64,512]{1,0:T(8,128)}), f32[64,512]{1,0:T(8,128)}) %all-reduce.3.cloned.1.call-update) | async-done | bytes 131088 | tf_op jit(solution)/shard_map/while/body/eval_jaxpr/psum | solution.py:66
  702.5 3.1 convolution_select_fusion.2
  705.6 34.1 %all-reduce.5.cloned.1.call-done = f32[64,512]{1,0:T(8,128)} async-done(((f32[64,512]{1,0:T(8,128)}), f32[64,512]{1,0:T(8,128)}) %all-reduce.5.cloned.1.call-update) | async-done | bytes 131088 | tf_op jit(solution)/shard_map/while/body/eval_jaxpr/psum | solution.py:9
  742.7 54.8 %all-reduce.3.cloned.1.call-done = f32[64,512]{1,0:T(8,128)} async-done(((f32[64,512]{1,0:T(8,128)}), f32[64,512]{1,0:T(8,128)}) %all-reduce.3.cloned.1.call-update) | async-done | bytes 131088 | tf_op jit(solution)/shard_map/while/body/eval_jaxpr/psum | solution.py:66
  797.5 3.1 convolution_select_fusion.2
  800.6 34.1 %all-reduce.5.cloned.1.call-done = f32[64,512]{1,0:T(8,128)} async-done(((f32[64,512]{1,0:T(8,128)}), f32[64,512]{1,0:T(8,128)}) %all-reduce.5.cloned.1.call-update) | async-done | bytes 131088 | tf_op jit(solution)/shard_map/while/body/eval_jaxpr/psum | solution.py:9
  (81 shorter events, 32.4 us)
Async XLA Ops:
  6.5 51.1 %reduce-scatter.2.cloned.1.call-start = ((), (), s32[]{:S(2)}) async-start(), calls=%async_computation.1 | async-start | bytes 1310720 | tf_op jit(solution)/shard_map/reduce_scatter | solution.py:40
  57.6 1.7 collective-permute-start
  60.4 8.4 collective-permute-start.1
  68.8 7.6 collective-permute-start.2
  76.4 55.8 %all-reduce.3.cloned.1.call-start = ((), (), s32[]{:S(2)}) async-start(), calls=%async_computation.2 | async-start | bytes 262144 | tf_op jit(solution)/shard_map/while/body/eval_jaxpr/psum | solution.py:66
  78.3 91.2 %all-reduce.5.cloned.1.call-start = ((), (), s32[]{:S(2)}) async-start(), calls=%async_computation.3 | async-start | bytes 262144 | tf_op jit(solution)/shard_map/while/body/eval_jaxpr/psum | solution.py:9
  170.6 56.7 %all-reduce.3.cloned.1.call-start = ((), (), s32[]{:S(2)}) async-start(), calls=%async_computation.2 | async-start | bytes 262144 | tf_op jit(solution)/shard_map/while/body/eval_jaxpr/psum | solution.py:66
  172.4 92.1 %all-reduce.5.cloned.1.call-start = ((), (), s32[]{:S(2)}) async-start(), calls=%async_computation.3 | async-start | bytes 262144 | tf_op jit(solution)/shard_map/while/body/eval_jaxpr/psum | solution.py:9
  265.5 56.7 %all-reduce.3.cloned.1.call-start = ((), (), s32[]{:S(2)}) async-start(), calls=%async_computation.2 | async-start | bytes 262144 | tf_op jit(solution)/shard_map/while/body/eval_jaxpr/psum | solution.py:66
  267.4 92.1 %all-reduce.5.cloned.1.call-start = ((), (), s32[]{:S(2)}) async-start(), calls=%async_computation.3 | async-start | bytes 262144 | tf_op jit(solution)/shard_map/while/body/eval_jaxpr/psum | solution.py:9
  360.5 57.0 %all-reduce.3.cloned.1.call-start = ((), (), s32[]{:S(2)}) async-start(), calls=%async_computation.2 | async-start | bytes 262144 | tf_op jit(solution)/shard_map/while/body/eval_jaxpr/psum | solution.py:66
  362.4 92.4 %all-reduce.5.cloned.1.call-start = ((), (), s32[]{:S(2)}) async-start(), calls=%async_computation.3 | async-start | bytes 262144 | tf_op jit(solution)/shard_map/while/body/eval_jaxpr/psum | solution.py:9
  455.8 56.7 %all-reduce.3.cloned.1.call-start = ((), (), s32[]{:S(2)}) async-start(), calls=%async_computation.2 | async-start | bytes 262144 | tf_op jit(solution)/shard_map/while/body/eval_jaxpr/psum | solution.py:66
  457.7 92.1 %all-reduce.5.cloned.1.call-start = ((), (), s32[]{:S(2)}) async-start(), calls=%async_computation.3 | async-start | bytes 262144 | tf_op jit(solution)/shard_map/while/body/eval_jaxpr/psum | solution.py:9
  550.8 56.7 %all-reduce.3.cloned.1.call-start = ((), (), s32[]{:S(2)}) async-start(), calls=%async_computation.2 | async-start | bytes 262144 | tf_op jit(solution)/shard_map/while/body/eval_jaxpr/psum | solution.py:66
  552.7 92.1 %all-reduce.5.cloned.1.call-start = ((), (), s32[]{:S(2)}) async-start(), calls=%async_computation.3 | async-start | bytes 262144 | tf_op jit(solution)/shard_map/while/body/eval_jaxpr/psum | solution.py:9
  645.8 56.7 %all-reduce.3.cloned.1.call-start = ((), (), s32[]{:S(2)}) async-start(), calls=%async_computation.2 | async-start | bytes 262144 | tf_op jit(solution)/shard_map/while/body/eval_jaxpr/psum | solution.py:66
  647.7 92.1 %all-reduce.5.cloned.1.call-start = ((), (), s32[]{:S(2)}) async-start(), calls=%async_computation.3 | async-start | bytes 262144 | tf_op jit(solution)/shard_map/while/body/eval_jaxpr/psum | solution.py:9
  740.8 56.7 %all-reduce.3.cloned.1.call-start = ((), (), s32[]{:S(2)}) async-start(), calls=%async_computation.2 | async-start | bytes 262144 | tf_op jit(solution)/shard_map/while/body/eval_jaxpr/psum | solution.py:66
  742.7 92.1 %all-reduce.5.cloned.1.call-start = ((), (), s32[]{:S(2)}) async-start(), calls=%async_computation.3 | async-start | bytes 262144 | tf_op jit(solution)/shard_map/while/body/eval_jaxpr/psum | solution.py:9
  835.7 0.7 copy-start
Sparse Core Ops, SparseCore 0:
  27.6 29.9 reduce-scatter.1
  80.3 51.9 all-reduce.2
  135.5 34.0 all-reduce.4
  174.1 53.1 all-reduce.2
  230.5 34.0 all-reduce.4
  269.1 53.1 all-reduce.2
  325.5 34.0 all-reduce.4
  364.4 53.1 all-reduce.2
  420.8 34.0 all-reduce.4
  459.4 53.1 all-reduce.2
  515.7 34.0 all-reduce.4
  554.3 53.1 all-reduce.2
  610.7 34.0 all-reduce.4
  649.3 53.1 all-reduce.2
  705.7 34.0 all-reduce.4
  744.3 53.1 all-reduce.2
  800.7 34.0 all-reduce.4
